TPU v7x, 32 devices: a whole 2x2x4 slice. The times are simulated.
32 devices in a mesh: dp: 8 (over y, x, core), tensor: 4 (over z).
Axes of the slice: x: 2, y: 2, z: 4, core: 2. Of those that a mesh axis runs over, the one named last changes fastest.
Arguments:
- images: bfloat16 [32, 320, 1024], P('dp', None, 'tensor'), may hold values from -6 to 6
- lengths: int32 [32], P('dp'), may hold values from 224 to 320, as said below
- cotangent: bfloat16 [32, 320, 1024], P('dp', None, 'tensor'), may hold values from -6 to 6
- norm1_gain: float32 [1024], replicated, may hold values from 0.5 to 1.5
- norm1_shift: float32 [1024], replicated, may hold values from -1.75 to 1.75
- w_qkv: bfloat16 [1024, 3, 1024], P(None, None, 'tensor'), may hold values from -0.1875 to 0.1875
- qv_bias: float32 [2, 1024], P(None, 'tensor'), may hold values from -3 to 3
- w_proj: bfloat16 [1024, 1024], P('tensor'), may hold values from -1.5 to 1.5
- proj_bias: float32 [1024], replicated, may hold values from -3 to 3
- norm2_gain: float32 [1024], replicated, may hold values from 0.5 to 1.5
- norm2_shift: float32 [1024], replicated, may hold values from -1.75 to 1.75
- w_fc1: bfloat16 [1024, 4096], P(None, 'tensor'), may hold values from -0.1875 to 0.1875
- fc1_bias: float32 [4096], P('tensor'), may hold values from -3 to 3
- w_fc2: bfloat16 [4096, 1024], P('tensor'), may hold values from -0.09375 to 0.09375
- fc2_bias: float32 [1024], replicated, may hold values from -3 to 3
Outputs:
- output: bfloat16 [32, 320, 1024], P('dp', None, 'tensor')
- input_grad: bfloat16 [32, 320, 1024], P('dp', None, 'tensor')
- grad_norm1_gain: float32 [1024], replicated
- grad_norm1_shift: float32 [1024], replicated
- grad_w_qkv: float32 [1024, 3, 1024], P(None, None, 'tensor')
- grad_qv_bias: float32 [2, 1024], P(None, 'tensor')
- grad_w_proj: float32 [1024, 1024], P('tensor')
- grad_proj_bias: float32 [1024], replicated
- grad_norm2_gain: float32 [1024], replicated
- grad_norm2_shift: float32 [1024], replicated
- grad_w_fc1: float32 [1024, 4096], P(None, 'tensor')
- grad_fc1_bias: float32 [4096], P('tensor')
- grad_w_fc2: float32 [4096, 1024], P('tensor')
- grad_fc2_bias: float32 [1024], replicated
Inputs may be any that keep to these rules, and one draw needn't show every extreme that they name: lengths[i] is the number of valid slots of image i, which come first; some image has all 320 slots valid in every draw.
All inputs are finite; a program needn't handle non-finite values.
Results may differ from a plain program's by a relative error of at most 0.02.
Values may be sent and summed in bfloat16 or wider, within the bound.
A program may use at most 192 MiB of HBM per device.

v0:
```python
import jax
import jax.numpy as jnp
from jax import lax
from jax.sharding import PartitionSpec as P

HEAD_DIM = 64
EPS = 1e-06
MASKED = -1e30


def norm_rows(values, gain_row, shift_row):
    row_mean = jnp.mean(values, axis=-1, keepdims=True)
    centered = values - row_mean
    spread = jnp.mean(centered * centered, axis=-1, keepdims=True)
    inverse = lax.rsqrt(spread + EPS)
    unit_rows = centered * inverse
    return (unit_rows * gain_row + shift_row, unit_rows, inverse)


def norm_back(gradient, unit_rows, inverse, gain_row):
    scaled = gradient * gain_row
    first_mean = jnp.mean(scaled, axis=-1, keepdims=True)
    cross_mean = jnp.mean(scaled * unit_rows, axis=-1, keepdims=True)
    return inverse * (scaled - first_mean - unit_rows * cross_mean)


def scores_of(queries, key_heads, key_mask, score_scale):
    raw_scores = (
        jnp.einsum("bqhe,bkhe->bhqk", queries, key_heads, preferred_element_type=jnp.float32)
        * score_scale
    )
    return jnp.where(key_mask, raw_scores, MASKED)


def exact_gelu(values):
    return jax.nn.gelu(values, approximate=False)


def swap_with(values, axis, size, stride):
    return lax.ppermute(values, axis, [(i, i ^ stride) for i in range(size)])


def halving_sum(blocks, axis, size):
    me = lax.axis_index(axis)
    steps = size.bit_length() - 1
    assert 1 << steps == size
    held = [block.astype(jnp.float32) for block in blocks]
    for step in range(steps):
        bit = me >> step & 1
        kept, given = ([], [])
        for block in held:
            half = block.shape[0] // 2
            kept.append(lax.dynamic_slice_in_dim(block, bit * half, half, 0))
            given.append(
                lax.dynamic_slice_in_dim(block, (1 - bit) * half, half, 0).astype(jnp.bfloat16)
            )
        got = swap_with(tuple(given), axis, size, 1 << step)
        held = [mine + theirs.astype(jnp.float32) for mine, theirs in zip(kept, got)]
    held = [block.astype(jnp.bfloat16) for block in held]
    for step in reversed(range(steps)):
        bit = me >> step & 1
        got = swap_with(tuple(held), axis, size, 1 << step)
        held = [
            jnp.where(bit == 0, jnp.concatenate([mine, theirs]), jnp.concatenate([theirs, mine]))
            for mine, theirs in zip(held, got)
        ]
    return [block.astype(jnp.float32) for block in held]


def doubling_sum(values, axis, size):
    steps = size.bit_length() - 1
    assert 1 << steps == size
    values = [value.astype(jnp.bfloat16) for value in values]
    for step in range(steps):
        got = swap_with(tuple(values), axis, size, 1 << step)
        values = [
            (mine.astype(jnp.float32) + theirs.astype(jnp.float32)).astype(jnp.bfloat16)
            for mine, theirs in zip(values, got)
        ]
    return [value.astype(jnp.float32) for value in values]


def per_device(
    images,
    lengths,
    cotangent,
    norm1_gain,
    norm1_shift,
    w_qkv,
    qv_bias,
    w_proj,
    proj_bias,
    norm2_gain,
    norm2_shift,
    w_fc1,
    fc1_bias,
    w_fc2,
    fc2_bias,
):
    images_here, slot_count, col_count = images.shape
    model_width = w_qkv.shape[0]
    local_width = w_qkv.shape[2]
    heads_here = local_width // HEAD_DIM
    row_count = images_here * slot_count
    score_scale = HEAD_DIM ** (-0.5)
    first_col = lax.axis_index("tensor") * col_count
    full_images, full_cot = (
        lax.all_gather(images, "tensor", axis=2, tiled=True),
        lax.all_gather(cotangent, "tensor", axis=2, tiled=True),
    )
    slot_ids = jnp.arange(slot_count, dtype=jnp.int32)
    valid_slots = (slot_ids[None, :] < lengths[:, None]).astype(jnp.float32)
    keep_rows = valid_slots.reshape(row_count, 1)
    row_values = full_images.reshape(row_count, model_width).astype(jnp.float32) * keep_rows
    normed1, unit1, inverse1 = norm_rows(row_values, norm1_gain, norm1_shift)
    normed1 = normed1.astype(jnp.bfloat16)
    qkv_bias = jnp.concatenate([qv_bias[0], jnp.zeros_like(qv_bias[0]), qv_bias[1]])
    w_flat = w_qkv.reshape(model_width, 3 * local_width)
    qkv_rows = (jnp.dot(normed1, w_flat, preferred_element_type=jnp.float32) + qkv_bias).astype(
        jnp.bfloat16
    )
    qkv_rows = qkv_rows.reshape(images_here, slot_count, 3, heads_here, HEAD_DIM)
    queries = qkv_rows[:, :, 0]
    key_heads = qkv_rows[:, :, 1]
    value_heads = qkv_rows[:, :, 2]
    key_mask = valid_slots[:, None, None, :] > 0
    scores = scores_of(queries, key_heads, key_mask, score_scale)
    row_top = jnp.max(scores, axis=-1, keepdims=True)
    shifted = jnp.exp(scores - row_top)
    row_total = jnp.sum(shifted, axis=-1, keepdims=True)
    probability = (shifted / row_total).astype(jnp.bfloat16)
    log_total = row_top + jnp.log(row_total)
    mixed = jnp.einsum(
        "bhqk,bkhe->bqhe", probability, value_heads, preferred_element_type=jnp.float32
    ).astype(jnp.bfloat16)
    mixed_rows = mixed.reshape(row_count, local_width)
    attn_part = jnp.dot(mixed_rows, w_proj, preferred_element_type=jnp.float32)
    middle = (
        row_values
        + lax.psum(attn_part.astype(jnp.bfloat16), "tensor").astype(jnp.float32)
        + proj_bias
    )
    normed2, unit2, inverse2 = norm_rows(middle, norm2_gain, norm2_shift)
    normed2 = normed2.astype(jnp.bfloat16)
    pre_act = jnp.dot(normed2, w_fc1, preferred_element_type=jnp.float32) + fc1_bias
    activated = exact_gelu(pre_act).astype(jnp.bfloat16)
    ff_part = jnp.dot(activated, w_fc2, preferred_element_type=jnp.float32).astype(jnp.bfloat16)
    grad_out = full_cot.reshape(row_count, model_width).astype(jnp.float32) * keep_rows
    grad_ff = grad_out.astype(jnp.bfloat16)
    grad_fc2_bias = jnp.sum(grad_ff, axis=0, dtype=jnp.float32)
    grad_w_fc2 = jnp.einsum("rf,rd->fd", activated, grad_ff, preferred_element_type=jnp.float32)
    grad_act = jnp.einsum("rd,fd->rf", grad_ff, w_fc2, preferred_element_type=jnp.float32)
    gelu_pull = jax.vjp(exact_gelu, pre_act)[1]
    grad_pre = gelu_pull(grad_act)[0].astype(jnp.bfloat16)
    grad_fc1_bias = jnp.sum(grad_pre, axis=0, dtype=jnp.float32)
    grad_w_fc1 = jnp.einsum("rd,rf->df", normed2, grad_pre, preferred_element_type=jnp.float32)
    hidden_part = jnp.einsum("rf,df->rd", grad_pre, w_fc1, preferred_element_type=jnp.float32)
    grad_normed2 = lax.psum(hidden_part.astype(jnp.bfloat16), "tensor").astype(jnp.float32)
    ff_part, grad_normed2 = lax.optimization_barrier((ff_part, grad_normed2))
    ff_share = lax.psum_scatter(ff_part, "tensor", scatter_dimension=1, tiled=True).astype(
        jnp.float32
    )
    middle_cols = lax.dynamic_slice_in_dim(middle, first_col, col_count, 1)
    bias_cols = lax.dynamic_slice_in_dim(fc2_bias, first_col, col_count, 0)
    output = ((middle_cols + ff_share + bias_cols) * keep_rows).astype(jnp.bfloat16)
    output = output.reshape(images_here, slot_count, col_count)
    dp_size = lax.axis_size("dp")
    tensor_size = lax.axis_size("tensor")
    grad_norm2_gain = jnp.sum(grad_normed2 * unit2, axis=0)
    grad_norm2_shift = jnp.sum(grad_normed2, axis=0)
    grad_middle = grad_out + norm_back(grad_normed2, unit2, inverse2, norm2_gain)
    grad_attn = grad_middle.astype(jnp.bfloat16)
    grad_proj_bias = jnp.sum(grad_attn, axis=0, dtype=jnp.float32)
    grad_w_proj = jnp.einsum("rc,rd->cd", mixed_rows, grad_attn, preferred_element_type=jnp.float32)
    grad_w_fc1, grad_w_fc2, grad_w_proj = halving_sum(
        [grad_w_fc1, grad_w_fc2, grad_w_proj], "dp", dp_size
    )
    grad_fc1_bias, grad_fc2_bias, grad_proj_bias, grad_norm2_gain, grad_norm2_shift = doubling_sum(
        [grad_fc1_bias, grad_fc2_bias, grad_proj_bias, grad_norm2_gain, grad_norm2_shift],
        "dp",
        dp_size,
    )
    grad_mixed = jnp.einsum(
        "rd,cd->rc", grad_attn, w_proj, preferred_element_type=jnp.float32
    ).astype(jnp.bfloat16)
    grad_mixed = grad_mixed.reshape(images_here, slot_count, heads_here, HEAD_DIM)
    scores_again = scores_of(queries, key_heads, key_mask, score_scale)
    weights_soft = jnp.exp(scores_again - log_total)
    grad_value = jnp.einsum(
        "bhqk,bqhe->bkhe",
        weights_soft.astype(jnp.bfloat16),
        grad_mixed,
        preferred_element_type=jnp.float32,
    )
    grad_prob = jnp.einsum(
        "bqhe,bkhe->bhqk", grad_mixed, value_heads, preferred_element_type=jnp.float32
    )
    row_dot = jnp.sum(weights_soft * grad_prob, axis=-1, keepdims=True)
    grad_scores = (weights_soft * (grad_prob - row_dot)).astype(jnp.bfloat16)
    grad_query = (
        jnp.einsum("bhqk,bkhe->bqhe", grad_scores, key_heads, preferred_element_type=jnp.float32)
        * score_scale
    )
    grad_key = (
        jnp.einsum("bhqk,bqhe->bkhe", grad_scores, queries, preferred_element_type=jnp.float32)
        * score_scale
    )
    grad_qkv = jnp.stack([grad_query, grad_key, grad_value], axis=2).astype(jnp.bfloat16)
    grad_qkv = grad_qkv.reshape(row_count, 3 * local_width)
    bias_sums = jnp.sum(grad_qkv, axis=0, dtype=jnp.float32).reshape(3, local_width)
    grad_qv_bias = jnp.stack([bias_sums[0], bias_sums[2]])
    grad_w_qkv = jnp.einsum("rd,rc->dc", normed1, grad_qkv, preferred_element_type=jnp.float32)
    (grad_w_qkv,) = halving_sum([grad_w_qkv], "dp", dp_size)
    grad_w_qkv = grad_w_qkv.reshape(model_width, 3, local_width)
    normed_part = jnp.einsum(
        "rc,dc->rd", grad_qkv, w_flat, preferred_element_type=jnp.float32
    ).astype(jnp.bfloat16)
    output, normed_part = lax.optimization_barrier((output, normed_part))
    grad_normed1 = lax.psum_scatter(normed_part, "tensor", scatter_dimension=1, tiled=True).astype(
        jnp.float32
    )
    term = normed_part.astype(jnp.float32)
    term_gain = term * norm1_gain
    first_stat = jnp.sum(term_gain, axis=1)
    second_stat = jnp.sum(term_gain * unit1, axis=1)
    norm1_terms = jnp.stack([jnp.sum(term * unit1, axis=0), jnp.sum(term, axis=0)])
    first_stat, second_stat, norm1_terms = doubling_sum(
        [first_stat, second_stat, norm1_terms], "tensor", tensor_size
    )
    norm1_sums, grad_qv_bias = doubling_sum([norm1_terms, grad_qv_bias], "dp", dp_size)
    first_mean = first_stat / model_width
    second_mean = second_stat / model_width
    unit1_cols = lax.dynamic_slice_in_dim(unit1, first_col, col_count, 1)
    gain1_cols = lax.dynamic_slice_in_dim(norm1_gain, first_col, col_count, 0)
    input_part = inverse1 * (
        grad_normed1 * gain1_cols - first_mean[:, None] - unit1_cols * second_mean[:, None]
    )
    middle_grad_cols = lax.dynamic_slice_in_dim(grad_middle, first_col, col_count, 1)
    grad_input = (middle_grad_cols + input_part) * keep_rows
    input_grad = grad_input.astype(jnp.bfloat16).reshape(images_here, slot_count, col_count)
    return (
        output,
        input_grad,
        norm1_sums[0],
        norm1_sums[1],
        grad_w_qkv,
        grad_qv_bias,
        grad_w_proj,
        grad_proj_bias,
        grad_norm2_gain,
        grad_norm2_shift,
        grad_w_fc1,
        grad_fc1_bias,
        grad_w_fc2,
        grad_fc2_bias,
    )


def solution(mesh):
    in_specs = (
        P("dp", None, "tensor"),
        P("dp"),
        P("dp", None, "tensor"),
        P(),
        P(),
        P(None, None, "tensor"),
        P(None, "tensor"),
        P("tensor", None),
        P(),
        P(),
        P(),
        P(None, "tensor"),
        P("tensor"),
        P("tensor", None),
        P(),
    )
    out_specs = (
        P("dp", None, "tensor"),
        P("dp", None, "tensor"),
        P(),
        P(),
        P(None, None, "tensor"),
        P(None, "tensor"),
        P("tensor", None),
        P(),
        P(),
        P(),
        P(None, "tensor"),
        P("tensor"),
        P("tensor", None),
        P(),
    )
    return jax.shard_map(
        per_device, mesh=mesh, in_specs=in_specs, out_specs=out_specs, check_vma=False
    )
```

profile of v0, /device:TPU:0, one launch (start us, length us, event | category | flops | bytes accessed | tf_op | source)
XLA Modules:
  0.0 557.9 jit_solution(11959580105190340628)
XLA Ops:
  10.2 2.6 copy.46
  12.8 54.3 %all-gather.3.cloned.1.call-done = bf16[4,320,1024]{2,1,0:T(8,128)(2,1)} async-done(((bf16[4,320,256]{2,1,0:T(8,128)(2,1)}), bf16[4,320,1024]{2,1,0:T(8,128)(2,1)}) %all-gather.3.cloned.1.call-update) | async-done | bytes 2621456 | tf_op jit(solution)/shard_map/all_gather | solution.py:108
  67.2 2.6 fusion.13
  69.8 2.8 multiply_reduce_fusion.4
  75.4 3.5 add_convert_fusion.3
  78.9 6.7 %reshape.273 = bf16[4,320,3,4,64]{4,3,2,1,0:T(4,128)(2,1)} reshape(bf16[1280,768]{1,0:T(8,128)(2,1)} %add_convert_fusion.3) | data formatting | bytes 3932160 | tf_op jit(solution)/shard_map/reshape | solution.py:122
  85.6 3.9 fusion.64
  89.5 2.4 copy.76
  91.9 2.5 copy.77
  94.4 3.2 copy.78
  97.6 3.2 fusion.19
  102.8 2.4 fusion.28
  106.8 2.1 reshape.266
  108.8 3.4 convolution_convert_fusion.1
  112.3 9.4 %all-gather.5.cloned.1.call-done = bf16[4,320,1024]{2,1,0:T(8,128)(2,1)} async-done(((bf16[4,320,256]{2,1,0:T(8,128)(2,1)}), bf16[4,320,1024]{2,1,0:T(8,128)(2,1)}) %all-gather.5.cloned.1.call-update) | async-done | bytes 2621456 | tf_op jit(solution)/shard_map/all_gather | solution.py:109
  121.8 2.3 fusion.20
  136.9 90.1 %all-reduce.3.cloned.1.call-done = bf16[1280,1024]{1,0:T(8,128)(2,1)} async-done(((bf16[1280,1024]{1,0:T(8,128)(2,1)}), bf16[1280,1024]{1,0:T(8,128)(2,1)}) %all-reduce.3.cloned.1.call-update) | async-done | bytes 2621456 | tf_op jit(solution)/shard_map/psum | solution.py:140
  227.0 5.0 fusion.63
  232.7 2.5 copy-done.45
  235.2 3.1 fusion.59
  238.3 16.9 %fusion.60 = (bf16[1024]{0:T(1024)(128)(2,1)}, bf16[1280,1024]{1,0:T(8,128)(2,1)}, f32[1280,1024]{1,0:T(8,128)S(1)}) fusion(f32[1280,1024]{1,0:T(8,128)S(1)} %fusion.59, f32[1024]{0:T(1024)S(1)} %copy-done.42, bf16[1280,1024]{1,0:T(8,128)(2,1)S(1)} %get-tuple-element.44, bf16[1024,1024]{1,0:T(8,128)(2,1)S(1)} %copy-done), kind=kOutput, calls=%fused_computation.180 | convolution fusion | flops 2781346816 | bytes 17831936 | tf_op jit(solution)/shard_map/rd,fd->rf/dot_general | solution.py:152
  256.6 2.9 fusion.68
  260.9 5.2 fusion.58
  266.1 4.2 convolution_convert_fusion.2
  270.9 2.7 dynamic-slice_convert_fusion.1
  273.6 6.3 %convolution_convert_fusion.3 = bf16[1280,1024]{1,0:T(8,128)(2,1)} fusion(bf16[1280,1024]{1,0:T(8,128)(2,1)} %copy-done.13, bf16[1024,1024]{1,0:T(8,128)(2,1)S(1)} %copy-done), kind=kOutput, calls=%fused_computation.56 | convolution fusion | flops 2685665280 | bytes 7340032 | tf_op jit(solution)/shard_map/dot_general | solution.py:147
  279.9 2.4 convert_add_fusion
  288.3 9.0 %collective-permute-done.43 = bf16[256,1024]{1,0:T(8,128)(2,1)S(1)} collective-permute-done((bf16[256,1024]{1,0:T(8,128)(2,1)S(1)}, bf16[256,1024]{1,0:T(8,128)(2,1)S(1)}, u32[]{:S(2)}, u32[]{:S(2)}) %collective-permute-start.43) | collective-permute-done | bytes 524320 | tf_op jit(solution)/shard_map/ppermute | solution.py:40
  298.8 9.4 %collective-permute-done.34 = bf16[256,1024]{1,0:T(8,128)(2,1)S(1)} collective-permute-done((bf16[256,1024]{1,0:T(8,128)(2,1)S(1)}, bf16[256,1024]{1,0:T(8,128)(2,1)S(1)}, u32[]{:S(2)}, u32[]{:S(2)}) %collective-permute-start.34) | collective-permute-done | bytes 524320 | tf_op jit(solution)/shard_map/ppermute | solution.py:40
  311.9 5.7 %collective-permute-done.35 = bf16[128,1024]{1,0:T(8,128)(2,1)S(1)} collective-permute-done((bf16[128,1024]{1,0:T(8,128)(2,1)S(1)}, bf16[128,1024]{1,0:T(8,128)(2,1)S(1)}, u32[]{:S(2)}, u32[]{:S(2)}) %collective-permute-start.35) | collective-permute-done | bytes 262176 | tf_op jit(solution)/shard_map/ppermute | solution.py:40
  319.6 3.7 collective-permute-done.45
  325.5 2.3 collective-permute-done.36
  329.9 44.2 %all-reduce.5.cloned.1.call-done = bf16[1280,1024]{1,0:T(8,128)(2,1)} async-done(((bf16[1280,1024]{1,0:T(8,128)(2,1)}), bf16[1280,1024]{1,0:T(8,128)(2,1)}) %all-reduce.5.cloned.1.call-update) | async-done | bytes 2621456 | tf_op jit(solution)/shard_map/psum | solution.py:158
  374.1 2.5 convert_element_type.548
  376.7 5.3 multiply_reduce_fusion.1
  382.0 3.0 convert_reduce_fusion
  385.1 2.3 fusion.51
  390.2 3.2 copy.54
  393.4 6.4 %fusion.29 = bf16[4,320,1,4,64]{1,4,3,0,2:T(8,128)(2,1)} fusion(bf16[4,320,4,64]{1,3,2,0:T(8,128)(2,1)} %copy.54, f32[4,4,320]{2,1,0:T(4,128)} %bitcast.109, f32[4,4,320,320]{2,3,1,0:T(8,128)} %copy-done.1, pred[4,320]{1,0:T(4,128)(4,1)S(1)} %copy-done.34), kind=kOutput, calls=%fused_computation.80 | convolution fusion | flops 216596480 | bytes 7886080 | tf_op jit(solution)/shard_map/bhqk,bqhe->bkhe/dot_general | solution.py:189
  399.8 5.4 multiply_reduce_fusion
  405.2 2.7 multiply_convert_fusion
  408.0 2.2 fusion.33
  412.7 3.2 fusion.62
  416.1 5.3 copy.59
  421.5 4.7 convert_element_type.555
  428.0 4.7 fusion.69
  435.3 3.8 convolution_convert_fusion
  439.6 2.2 maximum_select_fusion.4
  441.9 3.1 maximum_select_fusion.3
  461.6 3.4 collective-permute-done.19
  472.1 3.5 collective-permute-done.10
  478.1 2.6 multiply_convert_fusion.6
  480.7 3.0 collective-permute-done.11
  498.8 3.2 collective-permute-done.13
  504.9 4.4 fusion.22
  509.4 5.3 fusion.21
  517.5 2.3 copy.66
  519.8 2.2 reduce.7
  522.0 6.8 %fusion.5 = (bf16[1024]{0:T(1024)(128)(2,1)S(1)}, bf16[1280]{0:T(1024)(128)(2,1)S(1)}, bf16[1280]{0:T(1024)(128)(2,1)S(1)}, f32[1280,1024]{1,0:T(8,128)}) fusion(bf16[1280,1024]{1,0:T(8,128)(2,1)} %convolution_convert_fusion, f32[1280]{0:T(1024)S(1)} %copy-done.31, f32[1280]{0:T(1024)} %div.43, f32[1280]{0:T(1024)S(1)} %reshape.271, ...), kind=kLoop, calls=%fused_computation.14 | loop fusion | flops 14414336 | bytes 10512384 | tf_op jit(solution)/shard_map/reduce_sum | solution.py:226
  529.0 2.0 fusion.23
  531.0 2.0 collective-permute-start.2
  540.7 2.5 collective-permute-done.7
  543.3 3.6 collective-permute-done.8
  547.4 3.2 multiply_convert_fusion.5
  (303 shorter events, 109.5 us)
Async XLA Ops:
  7.2 231.1 %copy-start = (bf16[1024,1024]{1,0:T(8,128)(2,1)S(1)}, bf16[1024,1024]{1,0:T(8,128)(2,1)}, u32[]{:S(2)}) copy-start(bf16[1024,1024]{1,0:T(8,128)(2,1)} %param.28) | copy-start | bytes 6291460
  7.2 65.4 %copy-start.35 = (f32[1024]{0:T(1024)S(1)}, f32[1024]{0:T(1024)}, u32[]{:S(2)}) copy-start(f32[1024]{0:T(1024)} %param.18) | copy-start | bytes 12292
  7.2 65.3 %copy-start.41 = (f32[1024]{0:T(1024)S(1)}, f32[1024]{0:T(1024)}, u32[]{:S(2)}) copy-start(f32[1024]{0:T(1024)} %param.19) | copy-start | bytes 12292
  7.2 60.0 %all-gather.3.cloned.1.call-start = ((), (), s32[]{:S(2)}) async-start(), calls=%async_computation.2 | async-start | bytes 3276800 | tf_op jit(solution)/shard_map/all_gather | solution.py:108
  8.0 113.8 %all-gather.5.cloned.1.call-start = ((), (), s32[]{:S(2)}) async-start(), calls=%async_computation.4 | async-start | bytes 3276800 | tf_op jit(solution)/shard_map/all_gather | solution.py:109
  8.7 218.3 %all-reduce.3.cloned.1.call-start = ((), (), s32[]{:S(2)}) async-start(), calls=%async_computation.3 | async-start | bytes 5242880 | tf_op jit(solution)/shard_map/psum | solution.py:140
  10.2 92.5 %copy-start.33 = (pred[4,320]{1,0:T(4,128)(4,1)}, pred[4,320]{1,0:T(4,128)(4,1)S(1)}, u32[]{:S(2)}) copy-start(pred[4,320]{1,0:T(4,128)(4,1)S(1)} %get-tuple-element.49) | copy-start | bytes 3844
  112.3 261.8 %all-reduce.5.cloned.1.call-start = ((), (), s32[]{:S(2)}) async-start(), calls=%async_computation.5 | async-start | bytes 5242880 | tf_op jit(solution)/shard_map/psum | solution.py:158
  124.1 1.2 collective-permute-start.48
  125.9 4.2 collective-permute-start.49
  130.8 5.6 collective-permute-start.50
  232.0 28.9 %copy-start.2 = (f32[1280,1024]{1,0:T(8,128)}, f32[1280,1024]{1,0:T(8,128)S(1)}, u32[]{:S(2)}) copy-start(f32[1280,1024]{1,0:T(8,128)S(1)} %get-tuple-element.37) | copy-start | bytes 15728644
  235.2 25.7 %copy-start.29 = (f32[1280]{0:T(1024)}, f32[1280]{0:T(1024)S(1)}, u32[]{:S(2)}) copy-start(f32[1280]{0:T(1024)S(1)} %add_rsqrt_fusion) | copy-start | bytes 15364
  260.9 19.0 %collective-permute-start.42 = (bf16[512,1024]{1,0:T(8,128)(2,1)}, bf16[512,1024]{1,0:T(8,128)(2,1)}, u32[]{:S(2)}, u32[]{:S(2)}) collective-permute-start(bf16[512,1024]{1,0:T(8,128)(2,1)} %dynamic-slice_convert_fusion), channel_id=1, source_target_pairs={{0,4},{4,0},{8,12},{12,8},{16,20},{20,16},{24,28},{28,24},{1,5},{5... | collective-permute-start | bytes 3145736 | tf_op jit(solution)/shard_map/ppermute | solution.py:40
  270.3 16.0 %collective-permute-start.39 = (bf16[1024]{0:T(1024)(128)(2,1)}, bf16[1024]{0:T(1024)(128)(2,1)}, u32[]{:S(2)}, u32[]{:S(2)}) collective-permute-start(bf16[1024]{0:T(1024)(128)(2,1)} %get-tuple-element.29), channel_id=1, source_target_pairs={{0,4},{4,0},{8,12},{12,8},{16,20},{20,16},{24,28},{28,24},{1,5},{5... | collective-permute-start | bytes 6152 | tf_op jit(solution)/shard_map/ppermute | solution.py:40
  270.8 207.2 %reduce-scatter.3.cloned.1.call-start = ((), (), s32[]{:S(2)}) async-start(), calls=%async_computation.6 | async-start | bytes 3276800 | tf_op jit(solution)/shard_map/reduce_scatter | solution.py:160
  273.6 10.1 %collective-permute-start.33 = (bf16[512,1024]{1,0:T(8,128)(2,1)}, bf16[512,1024]{1,0:T(8,128)(2,1)}, u32[]{:S(2)}, u32[]{:S(2)}) collective-permute-start(bf16[512,1024]{1,0:T(8,128)(2,1)} %dynamic-slice_convert_fusion.1), channel_id=1, source_target_pairs={{0,4},{4,0},{8,12},{12,8},{16,20},{20,16},{24,28},{28,24},{1,5},{5... | collective-permute-start | bytes 3145736 | tf_op jit(solution)/shard_map/ppermute | solution.py:40
  282.4 14.9 %collective-permute-start.43 = (bf16[256,1024]{1,0:T(8,128)(2,1)S(1)}, bf16[256,1024]{1,0:T(8,128)(2,1)S(1)}, u32[]{:S(2)}, u32[]{:S(2)}) collective-permute-start(bf16[256,1024]{1,0:T(8,128)(2,1)S(1)} %dynamic-slice_convert_fusion.3), channel_id=1, source_target_pairs={{0,8},{4,12},{8,0},{12,4},{16,24},{20,28},{24,16},{28,20},{1,9},{5... | collective-permute-start | bytes 1572872 | tf_op jit(solution)/shard_map/ppermute | solution.py:40
  285.5 22.6 %collective-permute-start.34 = (bf16[256,1024]{1,0:T(8,128)(2,1)S(1)}, bf16[256,1024]{1,0:T(8,128)(2,1)S(1)}, u32[]{:S(2)}, u32[]{:S(2)}) collective-permute-start(bf16[256,1024]{1,0:T(8,128)(2,1)S(1)} %dynamic-slice_convert_fusion.4), channel_id=1, source_target_pairs={{0,8},{4,12},{8,0},{12,4},{16,24},{20,28},{24,16},{28,20},{1,9},{5... | collective-permute-start | bytes 1572872 | tf_op jit(solution)/shard_map/ppermute | solution.py:40
  287.1 22.7 %collective-permute-start.40 = (bf16[1024]{0:T(1024)(128)(2,1)S(1)}, bf16[1024]{0:T(1024)(128)(2,1)S(1)}, u32[]{:S(2)}, u32[]{:S(2)}) collective-permute-start(bf16[1024]{0:T(1024)(128)(2,1)S(1)} %add_convert_fusion.22), channel_id=1, source_target_pairs={{0,8},{4,12},{8,0},{12,4},{16,24},{20,28},{24,16},{28,20},{1,9},{5... | collective-permute-start | bytes 6152 | tf_op jit(solution)/shard_map/ppermute | solution.py:40
  297.5 13.1 %collective-permute-start.44 = (bf16[128,1024]{1,0:T(8,128)(2,1)S(1)}, bf16[128,1024]{1,0:T(8,128)(2,1)S(1)}, u32[]{:S(2)}, u32[]{:S(2)}) collective-permute-start(bf16[128,1024]{1,0:T(8,128)(2,1)S(1)} %dynamic-slice_convert_fusion.6), channel_id=1, source_target_pairs={{0,16},{4,20},{8,24},{12,28},{16,0},{20,4},{24,8},{28,12},{1,17},{... | collective-permute-start | bytes 786440 | tf_op jit(solution)/shard_map/ppermute | solution.py:40
  308.4 9.2 %collective-permute-start.35 = (bf16[128,1024]{1,0:T(8,128)(2,1)S(1)}, bf16[128,1024]{1,0:T(8,128)(2,1)S(1)}, u32[]{:S(2)}, u32[]{:S(2)}) collective-permute-start(bf16[128,1024]{1,0:T(8,128)(2,1)S(1)} %dynamic-slice_convert_fusion.7), channel_id=1, source_target_pairs={{0,16},{4,20},{8,24},{12,28},{16,0},{20,4},{24,8},{28,12},{1,17},{... | collective-permute-start | bytes 786440 | tf_op jit(solution)/shard_map/ppermute | solution.py:40
  309.7 9.3 %collective-permute-start.41 = (bf16[1024]{0:T(1024)(128)(2,1)S(1)}, bf16[1024]{0:T(1024)(128)(2,1)S(1)}, u32[]{:S(2)}, u32[]{:S(2)}) collective-permute-start(bf16[1024]{0:T(1024)(128)(2,1)S(1)} %add_convert_fusion.21), channel_id=1, source_target_pairs={{0,16},{4,20},{8,24},{12,28},{16,0},{20,4},{24,8},{28,12},{1,17},{... | collective-permute-start | bytes 6152 | tf_op jit(solution)/shard_map/ppermute | solution.py:40
  310.6 12.7 %collective-permute-start.45 = (bf16[128,1024]{1,0:T(8,128)(2,1)S(1)}, bf16[128,1024]{1,0:T(8,128)(2,1)S(1)}, u32[]{:S(2)}, u32[]{:S(2)}) collective-permute-start(bf16[128,1024]{1,0:T(8,128)(2,1)S(1)} %add_convert_fusion.4), channel_id=1, source_target_pairs={{0,16},{4,20},{8,24},{12,28},{16,0},{20,4},{24,8},{28,12},{1,17},{... | collective-permute-start | bytes 786440 | tf_op jit(solution)/shard_map/ppermute | solution.py:40
  317.7 10.1 %collective-permute-start.36 = (bf16[128,1024]{1,0:T(8,128)(2,1)S(1)}, bf16[128,1024]{1,0:T(8,128)(2,1)S(1)}, u32[]{:S(2)}, u32[]{:S(2)}) collective-permute-start(bf16[128,1024]{1,0:T(8,128)(2,1)S(1)} %add_convert_fusion.5), channel_id=1, source_target_pairs={{0,16},{4,20},{8,24},{12,28},{16,0},{20,4},{24,8},{28,12},{1,17},{... | collective-permute-start | bytes 786440 | tf_op jit(solution)/shard_map/ppermute | solution.py:40
  324.2 114.9 %collective-permute-start.46 = (bf16[256,1024]{1,0:T(8,128)(2,1)}, bf16[256,1024]{1,0:T(8,128)(2,1)}, u32[]{:S(2)}, u32[]{:S(2)}) collective-permute-start(bf16[256,1024]{1,0:T(8,128)(2,1)} %maximum_select_fusion.9), channel_id=1, source_target_pairs={{0,8},{4,12},{8,0},{12,4},{16,24},{20,28},{24,16},{28,20},{1,9},{5... | collective-permute-start | bytes 1572872 | tf_op jit(solution)/shard_map/ppermute | solution.py:40
  328.7 113.0 %collective-permute-start.37 = (bf16[256,1024]{1,0:T(8,128)(2,1)}, bf16[256,1024]{1,0:T(8,128)(2,1)}, u32[]{:S(2)}, u32[]{:S(2)}) collective-permute-start(bf16[256,1024]{1,0:T(8,128)(2,1)} %maximum_select_fusion.8), channel_id=1, source_target_pairs={{0,8},{4,12},{8,0},{12,4},{16,24},{20,28},{24,16},{28,20},{1,9},{5... | collective-permute-start | bytes 1572872 | tf_op jit(solution)/shard_map/ppermute | solution.py:40
  412.0 135.5 %reduce-scatter.5.cloned.1.call-start = ((), (), s32[]{:S(2)}) async-start(), calls=%async_computation.7 | async-start | bytes 3276800 | tf_op jit(solution)/shard_map/reduce_scatter | solution.py:219
  412.0 33.4 %collective-permute-start.24 = (bf16[1024]{0:T(1024)(128)(2,1)S(1)}, bf16[1024]{0:T(1024)(128)(2,1)S(1)}, u32[]{:S(2)}, u32[]{:S(2)}) collective-permute-start(bf16[1024]{0:T(1024)(128)(2,1)S(1)} %copy-done.40), channel_id=1, source_target_pairs={{0,4},{4,0},{8,12},{12,8},{16,20},{20,16},{24,28},{28,24},{1,5},{5... | collective-permute-start | bytes 6152 | tf_op jit(solution)/shard_map/ppermute | solution.py:40
  412.1 33.4 %collective-permute-start.27 = (bf16[1024]{0:T(1024)(128)(2,1)S(1)}, bf16[1024]{0:T(1024)(128)(2,1)S(1)}, u32[]{:S(2)}, u32[]{:S(2)}) collective-permute-start(bf16[1024]{0:T(1024)(128)(2,1)S(1)} %copy-done.39), channel_id=1, source_target_pairs={{0,4},{4,0},{8,12},{12,8},{16,20},{20,16},{24,28},{28,24},{1,5},{5... | collective-permute-start | bytes 6152 | tf_op jit(solution)/shard_map/ppermute | solution.py:40
  412.6 36.6 %collective-permute-start.30 = (bf16[1024]{0:T(1024)(128)(2,1)S(1)}, bf16[1024]{0:T(1024)(128)(2,1)S(1)}, u32[]{:S(2)}, u32[]{:S(2)}) collective-permute-start(bf16[1024]{0:T(1024)(128)(2,1)S(1)} %copy-done.38), channel_id=1, source_target_pairs={{0,4},{4,0},{8,12},{12,8},{16,20},{20,16},{24,28},{28,24},{1,5},{5... | collective-permute-start | bytes 6152 | tf_op jit(solution)/shard_map/ppermute | solution.py:40
  439.2 28.0 %copy-start.20 = (f32[1024,768]{0,1:T(8,128)S(1)}, f32[1024,768]{0,1:T(8,128)}, u32[]{:S(2)}) copy-start(f32[1024,768]{0,1:T(8,128)} %copy-done.19) | copy-start | bytes 9437188
  439.2 18.9 %collective-permute-start.18 = (bf16[128,1024]{1,0:T(8,128)(2,1)}, bf16[128,1024]{1,0:T(8,128)(2,1)S(1)}, u32[]{:S(2)}, u32[]{:S(2)}) collective-permute-start(bf16[128,1024]{1,0:T(8,128)(2,1)} %dynamic-slice_convert_fusion.8), channel_id=1, source_target_pairs={{0,4},{4,0},{8,12},{12,8},{16,20},{20,16},{24,28},{28,24},{1,5},{5... | collective-permute-start | bytes 786440 | tf_op jit(solution)/shard_map/ppermute | solution.py:40
  441.8 3.2 collective-permute-start.15
  445.0 21.7 %collective-permute-start.9 = (bf16[512,768]{0,1:T(8,128)(2,1)}, bf16[512,768]{0,1:T(8,128)(2,1)S(1)}, u32[]{:S(2)}, u32[]{:S(2)}) collective-permute-start(bf16[512,768]{0,1:T(8,128)(2,1)} %dynamic-slice_convert_fusion.2), channel_id=1, source_target_pairs={{0,4},{4,0},{8,12},{12,8},{16,20},{20,16},{24,28},{28,24},{1,5},{5... | collective-permute-start | bytes 2359304 | tf_op jit(solution)/shard_map/ppermute | solution.py:40
  445.4 59.5 %collective-permute-start.47 = (bf16[512,1024]{1,0:T(8,128)(2,1)S(1)}, bf16[512,1024]{1,0:T(8,128)(2,1)}, u32[]{:S(2)}, u32[]{:S(2)}) collective-permute-start(bf16[512,1024]{1,0:T(8,128)(2,1)S(1)} %maximum_select_fusion.4), channel_id=1, source_target_pairs={{0,4},{4,0},{8,12},{12,8},{16,20},{20,16},{24,28},{28,24},{1,5},{5... | collective-permute-start | bytes 3145736 | tf_op jit(solution)/shard_map/ppermute | solution.py:40
  445.6 3.6 collective-permute-start.16
  449.2 60.2 %collective-permute-start.38 = (bf16[512,1024]{1,0:T(8,128)(2,1)}, bf16[512,1024]{1,0:T(8,128)(2,1)}, u32[]{:S(2)}, u32[]{:S(2)}) collective-permute-start(bf16[512,1024]{1,0:T(8,128)(2,1)} %maximum_select_fusion.3), channel_id=1, source_target_pairs={{0,4},{4,0},{8,12},{12,8},{16,20},{20,16},{24,28},{28,24},{1,5},{5... | collective-permute-start | bytes 3145736 | tf_op jit(solution)/shard_map/ppermute | solution.py:40
  449.2 3.6 collective-permute-start.17
  452.9 3.6 collective-permute-start.25
  456.4 3.6 collective-permute-start.28
  458.0 9.5 %collective-permute-start.31 = (bf16[1024]{0:T(1024)(128)(2,1)S(1)}, bf16[1024]{0:T(1024)(128)(2,1)S(1)}, u32[]{:S(2)}, u32[]{:S(2)}) collective-permute-start(bf16[1024]{0:T(1024)(128)(2,1)S(1)} %add_convert_fusion.25), channel_id=1, source_target_pairs={{0,8},{4,12},{8,0},{12,4},{16,24},{20,28},{24,16},{28,20},{1,9},{5... | collective-permute-start | bytes 6152 | tf_op jit(solution)/shard_map/ppermute | solution.py:40
  460.0 5.0 collective-permute-start.19
  465.0 21.7 %collective-permute-start.26 = (bf16[1024]{0:T(1024)(128)(2,1)S(1)}, bf16[1024]{0:T(1024)(128)(2,1)}, u32[]{:S(2)}, u32[]{:S(2)}) collective-permute-start(bf16[1024]{0:T(1024)(128)(2,1)S(1)} %add_convert_fusion.30), channel_id=1, source_target_pairs={{0,16},{4,20},{8,24},{12,28},{16,0},{20,4},{24,8},{28,12},{1,17},{... | collective-permute-start | bytes 6152 | tf_op jit(solution)/shard_map/ppermute | solution.py:40
  466.6 4.3 collective-permute-start.20
  467.5 8.0 %collective-permute-start.10 = (bf16[256,768]{0,1:T(8,128)(2,1)S(1)}, bf16[256,768]{0,1:T(8,128)(2,1)S(1)}, u32[]{:S(2)}, u32[]{:S(2)}) collective-permute-start(bf16[256,768]{0,1:T(8,128)(2,1)S(1)} %dynamic-slice_convert_fusion.5), channel_id=1, source_target_pairs={{0,8},{4,12},{8,0},{12,4},{16,24},{20,28},{24,16},{28,20},{1,9},{5... | collective-permute-start | bytes 1179656 | tf_op jit(solution)/shard_map/ppermute | solution.py:40
  471.0 23.2 %collective-permute-start.29 = (bf16[1024]{0:T(1024)(128)(2,1)S(1)}, bf16[1024]{0:T(1024)(128)(2,1)}, u32[]{:S(2)}, u32[]{:S(2)}) collective-permute-start(bf16[1024]{0:T(1024)(128)(2,1)S(1)} %add_convert_fusion.27), channel_id=1, source_target_pairs={{0,16},{4,20},{8,24},{12,28},{16,0},{20,4},{24,8},{28,12},{1,17},{... | collective-permute-start | bytes 6152 | tf_op jit(solution)/shard_map/ppermute | solution.py:40
  476.6 7.1 %collective-permute-start.11 = (bf16[128,768]{0,1:T(8,128)(2,1)S(1)}, bf16[128,768]{0,1:T(8,128)(2,1)S(1)}, u32[]{:S(2)}, u32[]{:S(2)}) collective-permute-start(bf16[128,768]{0,1:T(8,128)(2,1)S(1)} %dynamic-slice_convert_fusion.9), channel_id=1, source_target_pairs={{0,16},{4,20},{8,24},{12,28},{16,0},{20,4},{24,8},{28,12},{1,17},{... | collective-permute-start | bytes 589832 | tf_op jit(solution)/shard_map/ppermute | solution.py:40
  483.7 4.5 collective-permute-start.21
  486.7 5.7 %collective-permute-start.12 = (bf16[128,768]{0,1:T(8,128)(2,1)S(1)}, bf16[128,768]{0,1:T(8,128)(2,1)S(1)}, u32[]{:S(2)}, u32[]{:S(2)}) collective-permute-start(bf16[128,768]{0,1:T(8,128)(2,1)S(1)} %add_convert_fusion.6), channel_id=1, source_target_pairs={{0,16},{4,20},{8,24},{12,28},{16,0},{20,4},{24,8},{28,12},{1,17},{... | collective-permute-start | bytes 589832 | tf_op jit(solution)/shard_map/ppermute | solution.py:40
  488.2 9.3 %collective-permute-start.32 = (bf16[1024]{0:T(1024)(128)(2,1)}, bf16[1024]{0:T(1024)(128)(2,1)S(1)}, u32[]{:S(2)}, u32[]{:S(2)}) collective-permute-start(bf16[1024]{0:T(1024)(128)(2,1)} %add_convert_fusion.24), channel_id=1, source_target_pairs={{0,16},{4,20},{8,24},{12,28},{16,0},{20,4},{24,8},{28,12},{1,17},{... | collective-permute-start | bytes 6152 | tf_op jit(solution)/shard_map/ppermute | solution.py:40
  492.4 5.0 collective-permute-start.22
  494.2 7.8 %collective-permute-start.13 = (bf16[256,768]{0,1:T(8,128)(2,1)S(1)}, bf16[256,768]{0,1:T(8,128)(2,1)S(1)}, u32[]{:S(2)}, u32[]{:S(2)}) collective-permute-start(bf16[256,768]{0,1:T(8,128)(2,1)S(1)} %maximum_select_fusion.11), channel_id=1, source_target_pairs={{0,8},{4,12},{8,0},{12,4},{16,24},{20,28},{24,16},{28,20},{1,9},{5... | collective-permute-start | bytes 1179656 | tf_op jit(solution)/shard_map/ppermute | solution.py:40
  497.4 6.4 %collective-permute-start.23 = (bf16[128,1024]{1,0:T(8,128)(2,1)S(1)}, bf16[128,1024]{1,0:T(8,128)(2,1)S(1)}, u32[]{:S(2)}, u32[]{:S(2)}) collective-permute-start(bf16[128,1024]{1,0:T(8,128)(2,1)S(1)} %maximum_select_fusion.12), channel_id=1, source_target_pairs={{0,4},{4,0},{8,12},{12,8},{16,20},{20,16},{24,28},{28,24},{1,5},{5... | collective-permute-start | bytes 786440 | tf_op jit(solution)/shard_map/ppermute | solution.py:40
  503.8 13.6 %collective-permute-start.14 = (bf16[512,768]{0,1:T(8,128)(2,1)}, bf16[512,768]{0,1:T(8,128)(2,1)}, u32[]{:S(2)}, u32[]{:S(2)}) collective-permute-start(bf16[512,768]{0,1:T(8,128)(2,1)} %maximum_select_fusion.6), channel_id=1, source_target_pairs={{0,4},{4,0},{8,12},{12,8},{16,20},{20,16},{24,28},{28,24},{1,5},{5... | collective-permute-start | bytes 2359304 | tf_op jit(solution)/shard_map/ppermute | solution.py:40
  528.9 4.2 collective-permute-start.4
  531.0 3.7 collective-permute-start.2
  533.0 4.7 collective-permute-start
  533.1 4.6 collective-permute-start.5
  534.7 5.9 %collective-permute-start.3 = (bf16[1280]{0:T(1024)(128)(2,1)S(1)}, bf16[1280]{0:T(1024)(128)(2,1)S(1)}, u32[]{:S(2)}, u32[]{:S(2)}) collective-permute-start(bf16[1280]{0:T(1024)(128)(2,1)S(1)} %add_convert_fusion.14), channel_id=1, source_target_pairs={{0,2},{1,3},{2,0},{3,1},{4,6},{5,7},{6,4},{7,5},{8,10},{9,11},{10,... | collective-permute-start | bytes 7688 | tf_op jit(solution)/shard_map/ppermute | solution.py:40
  537.6 1.8 collective-permute-start.6
  537.8 5.5 collective-permute-start.1
  539.5 3.7 collective-permute-start.7
  543.2 3.7 collective-permute-start.8
  (46 other events, 221.1 us)
Sparse Core Ops, SparseCore 0:
  9.6 57.5 all-gather.2
  68.7 52.9 all-gather.4
  124.7 102.2 all-reduce.2
  271.0 103.0 all-reduce.4
  412.1 51.3 reduce-scatter.2
  480.8 50.0 reduce-scatter.4
where the time goes:
time: 568 us; the launch traced here: 558 us
  waiting for transfers between devices  261 us (46%)
  other arithmetic  92.1 us (16%)
  matrix products  78.6 us (14%)
  local copies, waits for them, and re-layouts  64.3 us (11%)
  starting transfers between devices  46.3 us (8%)
  between operations  15.6 us (3%)
    psum x1, waiting for transfers between devices, per_device(): lax.psum(attn_part.astype(jnp.bfloat16), 'tensor').astype(jnp.float32)  90.1 us
    ppermute x51, waiting for transfers between devices, swap_with(): return lax.ppermute(values, axis, [(i, i ^ stride) for i in range(size)])  61.5 us
    all_gather x1, waiting for transfers between devices, per_device(): lax.all_gather(images, 'tensor', axis=2, tiled=True)  54.3 us
    ppermute x51, starting transfers between devices, swap_with(): return lax.ppermute(values, axis, [(i, i ^ stride) for i in range(size)])  46.1 us
    psum x1, waiting for transfers between devices, per_device(): lax.psum(hidden_part.astype(jnp.bfloat16), 'tensor').astype(jnp.float32)  44.2 us
    unnamed x110, local copies, waits for them, and re-layouts  18.4 us
    dot_general x1, matrix products, per_device(): jnp.einsum('rd,fd->rf', grad_ff, w_fc2, preferred_element_type=jnp.float32)  16.9 us
    convert_element_type x4, other arithmetic, halving_sum(): return [block.astype(jnp.float32) for block in held]  12.9 us
  transfers between devices with their start and end apart: 57, of which 24 were waited for; matrix products, arithmetic and copies ran while one was open for 35% of the time, Pallas kernels for 0%

commit v1 on v0

--- a/solution.py
+++ b/solution.py
@@ -6,6 +6,27 @@
 HEAD_DIM = 64
 EPS = 1e-06
 MASKED = -1e30
+
+
+def ring_gather(shard, axis, dim):
+    size, index, extent = (lax.axis_size(axis), lax.axis_index(axis), shard.shape[dim])
+    upward = [(i, (i + 1) % size) for i in range(size)]
+    downward = [(i, (i - 1) % size) for i in range(size)]
+    out = jnp.zeros((*shard.shape[:dim], size * extent, *shard.shape[dim + 1 :]), shard.dtype)
+    out = lax.dynamic_update_slice_in_dim(out, shard, index * extent, axis=dim)
+    from_left = from_right = shard
+    half = size // 2
+    for step in range(1, half + 1):
+        from_left = lax.ppermute(from_left, axis, upward)
+        out = lax.dynamic_update_slice_in_dim(
+            out, from_left, (index - step) % size * extent, axis=dim
+        )
+        if step < size - half:
+            from_right = lax.ppermute(from_right, axis, downward)
+            out = lax.dynamic_update_slice_in_dim(
+                out, from_right, (index + step) % size * extent, axis=dim
+            )
+    return out
 
 
 def norm_rows(values, gain_row, shift_row):
@@ -105,7 +126,7 @@
     score_scale = HEAD_DIM ** (-0.5)
     first_col = lax.axis_index("tensor") * col_count
     full_images, full_cot = (
-        lax.all_gather(images, "tensor", axis=2, tiled=True),
+        ring_gather(images, "tensor", 2),
         lax.all_gather(cotangent, "tensor", axis=2, tiled=True),
     )
     slot_ids = jnp.arange(slot_count, dtype=jnp.int32)

time: 568 us -> 586 us (1.032)
  waiting for transfers between devices: 261 us -> 281 us
  other arithmetic: 92.1 us -> 73.6 us
  starting transfers between devices: 46.3 us -> 63.7 us
    ppermute x0 -> x3, waiting for transfers between devices: none -> 54.8 us  [the longest x2 36.4 us: ring_gather(): from_left = lax.ppermute(from_left, axis, upward)]
    all_gather x1 -> x0, waiting for transfers between devices: 54.3 us -> none  [per_device(): lax.all_gather(images, 'tensor', axis=2, tiled=True)]
    ppermute x0 -> x3, starting transfers between devices: none -> 19.8 us  [the longest x2 17.7 us: ring_gather(): from_left = lax.ppermute(from_left, axis, upward)]
    psum x1, waiting for transfers between devices: 90.1 us -> 108 us  [per_device(): lax.psum(attn_part.astype(jnp.bfloat16), 'tensor').astype(jnp.float32)]
    all_gather x1, waiting for transfers between devices: 9.44 us -> 0.01 us  [per_device(): lax.all_gather(cotangent, 'tensor', axis=2, tiled=True)]
    ppermute x51, waiting for transfers between devices: 61.5 us -> 68.3 us  [swap_with(): return lax.ppermute(values, axis, [(i, i ^ stride) for i in range(size)])]
    unnamed x110 -> x122, local copies, waits for them, and re-layouts: 18.4 us -> 17.7 us
  transfers between devices with their start and end apart: 57 -> 59, of which waited for: 24 -> 26; matrix products, arithmetic and copies ran while one was open for 35% -> 27% of each run, Pallas kernels for 0% -> 0%
where the time goes in v1:
time: 586 us; the launch traced here: 577 us
  waiting for transfers between devices  281 us (48%)
  matrix products  82.1 us (14%)
  other arithmetic  73.6 us (13%)
  starting transfers between devices  63.7 us (11%)
  local copies, waits for them, and re-layouts  60.9 us (10%)
  between operations  15.6 us (3%)
    psum x1, waiting for transfers between devices, per_device(): lax.psum(attn_part.astype(jnp.bfloat16), 'tensor').astype(jnp.float32)  108 us
    ppermute x51, waiting for transfers between devices, swap_with(): return lax.ppermute(values, axis, [(i, i ^ stride) for i in range(size)])  68.3 us
    psum x1, waiting for transfers between devices, per_device(): lax.psum(hidden_part.astype(jnp.bfloat16), 'tensor').astype(jnp.float32)  49.5 us
    ppermute x51, starting transfers between devices, swap_with(): return lax.ppermute(values, axis, [(i, i ^ stride) for i in range(size)])  43.8 us
    ppermute x2, waiting for transfers between devices, ring_gather(): from_left = lax.ppermute(from_left, axis, upward)  36.4 us
    ppermute x1, waiting for transfers between devices, ring_gather(): from_right = lax.ppermute(from_right, axis, downward)  18.4 us
    unnamed x122, local copies, waits for them, and re-layouts  17.7 us
    ppermute x2, starting transfers between devices, ring_gather(): from_left = lax.ppermute(from_left, axis, upward)  17.7 us
  transfers between devices with their start and end apart: 59, of which 26 were waited for; matrix products, arithmetic and copies ran while one was open for 27% of the time, Pallas kernels for 0%

profile of v1, /device:TPU:0, one launch (start us, length us, event | category | flops | bytes accessed | tf_op | source)
XLA Modules:
  0.0 576.6 jit_solution(13429548602923048205)
XLA Ops:
  7.3 3.1 collective-permute-start
  10.4 2.1 collective-permute-start.1
  13.3 18.4 %collective-permute-done = bf16[4,320,256]{2,1,0:T(8,128)(2,1)S(1)} collective-permute-done((bf16[4,320,256]{2,1,0:T(8,128)(2,1)}, bf16[4,320,256]{2,1,0:T(8,128)(2,1)S(1)}, u32[]{:S(2)}, u32[]{:S(2)}) %collective-permute-start) | collective-permute-done | bytes 655392 | tf_op jit(solution)/shard_map/ppermute | solution.py:20
  31.7 14.6 %collective-permute-start.2 = (bf16[4,320,256]{2,1,0:T(8,128)(2,1)S(1)}, bf16[4,320,256]{2,1,0:T(8,128)(2,1)}, u32[]{:S(2)}, u32[]{:S(2)}) collective-permute-start(bf16[4,320,256]{2,1,0:T(8,128)(2,1)S(1)} %collective-permute-done), channel_id=1, source_target_pairs={{0,1},{1,2},{2,3},{3,0},{4,5},{5,6},{6,7},{7,4},{8,9},{9,10},{10,1... | collective-permute-start | bytes 1966088 | tf_op jit(solution)/shard_map/ppermute | solution.py:20
  46.3 2.6 copy.46
  49.5 18.4 %collective-permute-done.1 = bf16[4,320,256]{2,1,0:T(8,128)(2,1)} collective-permute-done((bf16[4,320,256]{2,1,0:T(8,128)(2,1)}, bf16[4,320,256]{2,1,0:T(8,128)(2,1)}, u32[]{:S(2)}, u32[]{:S(2)}) %collective-permute-start.1) | collective-permute-done | bytes 655392 | tf_op jit(solution)/shard_map/ppermute | solution.py:25
  69.1 18.0 %collective-permute-done.2 = bf16[4,320,256]{2,1,0:T(8,128)(2,1)} collective-permute-done((bf16[4,320,256]{2,1,0:T(8,128)(2,1)S(1)}, bf16[4,320,256]{2,1,0:T(8,128)(2,1)}, u32[]{:S(2)}, u32[]{:S(2)}) %collective-permute-start.2) | collective-permute-done | bytes 655392 | tf_op jit(solution)/shard_map/ppermute | solution.py:20
  92.9 3.5 add_convert_fusion.3
  96.4 6.7 %reshape.273 = bf16[4,320,3,4,64]{4,3,2,1,0:T(4,128)(2,1)} reshape(bf16[1280,768]{1,0:T(8,128)(2,1)} %add_convert_fusion.3) | data formatting | bytes 3932160 | tf_op jit(solution)/shard_map/reshape | solution.py:143
  103.1 3.9 fusion.64
  107.0 2.4 copy.76
  109.4 2.5 copy.77
  111.9 3.3 copy.78
  115.1 3.2 fusion.19
  120.3 2.4 fusion.28
  124.3 2.1 reshape.266
  126.3 3.4 convolution_convert_fusion.1
  136.0 107.9 %all-reduce.3.cloned.1.call-done = bf16[1280,1024]{1,0:T(8,128)(2,1)} async-done(((bf16[1280,1024]{1,0:T(8,128)(2,1)}), bf16[1280,1024]{1,0:T(8,128)(2,1)}) %all-reduce.3.cloned.1.call-update) | async-done | bytes 2621456 | tf_op jit(solution)/shard_map/psum | solution.py:161
  243.9 5.0 fusion.63
  249.7 2.5 copy-done.52
  252.2 3.0 fusion.59
  255.2 16.5 %fusion.60 = (bf16[1024]{0:T(1024)(128)(2,1)}, bf16[1280,1024]{1,0:T(8,128)(2,1)}, f32[1280,1024]{1,0:T(8,128)S(1)}) fusion(f32[1280,1024]{1,0:T(8,128)S(1)} %fusion.59, f32[1024]{0:T(1024)S(1)} %copy-done.47, bf16[1280,1024]{1,0:T(8,128)(2,1)S(1)} %get-tuple-element.44, bf16[1024,1024]{1,0:T(8,128)(2,1)S(1)} %copy-done), kind=kOutput, calls=%fused_computation.184 | convolution fusion | flops 2781346816 | bytes 17831936 | tf_op jit(solution)/shard_map/rd,fd->rf/dot_general | solution.py:173
  273.1 4.5 fusion.68
  277.6 4.5 convolution_convert_fusion.3
  282.2 6.9 %convolution_convert_fusion.2 = bf16[1280,1024]{1,0:T(8,128)(2,1)} fusion(bf16[1280,1024]{1,0:T(8,128)(2,1)} %get-tuple-element.30, bf16[1024,1024]{1,0:T(8,128)(2,1)} %param.26), kind=kOutput, calls=%fused_computation.55 | convolution fusion | flops 2685665280 | bytes 7340032 | tf_op jit(solution)/shard_map/rf,df->rd/dot_general | solution.py:178
  289.1 8.6 %fusion.58 = f32[1024,1024]{1,0:T(8,128)} fusion(bf16[1280,1024]{1,0:T(8,128)(2,1)} %get-tuple-element.30, f32[1280,1024]{1,0:T(8,128)} %copy-done.3, f32[1024]{0:T(1024)S(1)} %copy-done.54, f32[1024]{0:T(1024)S(1)} %copy-done.42, f32[1280]{0:T(1024)S(1)} %copy-done.32, f32[1280]{0:T(1024)S(1)} %copy-done.27), kind=kOutput, calls=%fused_computation.182 | convolution fusion | flops 2690908160 | bytes 12077056 | tf_op jit(solution)/shard_map/rd,rf->df/dot_general | solution.py:177
  308.4 2.4 convert_add_fusion
  314.2 11.5 %collective-permute-done.46 = bf16[256,1024]{1,0:T(8,128)(2,1)S(1)} collective-permute-done((bf16[256,1024]{1,0:T(8,128)(2,1)S(1)}, bf16[256,1024]{1,0:T(8,128)(2,1)S(1)}, u32[]{:S(2)}, u32[]{:S(2)}) %collective-permute-start.46) | collective-permute-done | bytes 524320 | tf_op jit(solution)/shard_map/ppermute | solution.py:61
  326.6 8.1 %collective-permute-done.37 = bf16[256,1024]{1,0:T(8,128)(2,1)S(1)} collective-permute-done((bf16[256,1024]{1,0:T(8,128)(2,1)S(1)}, bf16[256,1024]{1,0:T(8,128)(2,1)S(1)}, u32[]{:S(2)}, u32[]{:S(2)}) %collective-permute-start.37) | collective-permute-done | bytes 524320 | tf_op jit(solution)/shard_map/ppermute | solution.py:61
  337.7 6.4 %collective-permute-done.38 = bf16[128,1024]{1,0:T(8,128)(2,1)S(1)} collective-permute-done((bf16[128,1024]{1,0:T(8,128)(2,1)S(1)}, bf16[128,1024]{1,0:T(8,128)(2,1)S(1)}, u32[]{:S(2)}, u32[]{:S(2)}) %collective-permute-start.38) | collective-permute-done | bytes 262176 | tf_op jit(solution)/shard_map/ppermute | solution.py:61
  345.5 4.0 collective-permute-done.48
  354.7 49.5 %all-reduce.5.cloned.1.call-done = bf16[1280,1024]{1,0:T(8,128)(2,1)} async-done(((bf16[1280,1024]{1,0:T(8,128)(2,1)}), bf16[1280,1024]{1,0:T(8,128)(2,1)}) %all-reduce.5.cloned.1.call-update) | async-done | bytes 2621456 | tf_op jit(solution)/shard_map/psum | solution.py:179
  404.2 2.5 convert_element_type.548
  406.8 5.5 multiply_reduce_fusion.1
  412.3 3.0 convert_reduce_fusion
  415.3 2.4 fusion.51
  420.8 6.2 %fusion.29 = bf16[4,320,1,4,64]{1,4,3,0,2:T(8,128)(2,1)} fusion(bf16[4,320,4,64]{1,3,2,0:T(8,128)(2,1)S(1)} %copy.54, f32[4,4,320]{2,1,0:T(4,128)} %bitcast.109, f32[4,4,320,320]{2,3,1,0:T(8,128)} %copy-done.2, pred[4,320]{1,0:T(4,128)(4,1)S(1)} %copy-done.37), kind=kOutput, calls=%fused_computation.80 | convolution fusion | flops 216596480 | bytes 7886080 | tf_op jit(solution)/shard_map/bhqk,bqhe->bkhe/dot_general | solution.py:210
  427.0 5.4 multiply_reduce_fusion
  432.4 2.5 multiply_convert_fusion
  437.9 3.0 fusion.62
  441.1 5.4 copy.59
  446.5 4.9 convert_element_type.555
  451.5 4.7 fusion.69
  458.9 3.8 convolution_convert_fusion
  463.1 2.2 maximum_select_fusion.4
  465.4 3.1 maximum_select_fusion.3
  470.6 2.2 collective-permute-done.19
  474.2 2.2 collective-permute-done.20
  485.0 3.6 collective-permute-done.22
  495.0 4.1 collective-permute-done.13
  501.6 2.6 multiply_convert_fusion.6
  504.3 3.5 collective-permute-done.14
  518.0 2.1 collective-permute-done.25
  520.9 3.7 collective-permute-done.16
  526.0 4.4 fusion.22
  530.4 5.3 fusion.21
  536.7 2.3 copy.66
  539.0 2.2 reduce.7
  541.3 6.7 %fusion.5 = (bf16[1024]{0:T(1024)(128)(2,1)S(1)}, bf16[1280]{0:T(1024)(128)(2,1)S(1)}, bf16[1280]{0:T(1024)(128)(2,1)S(1)}, f32[1280,1024]{1,0:T(8,128)}) fusion(bf16[1280,1024]{1,0:T(8,128)(2,1)} %convolution_convert_fusion, f32[1280]{0:T(1024)S(1)} %copy-done.34, f32[1280]{0:T(1024)S(1)} %copy-done.38, f32[1280]{0:T(1024)S(1)} %reshape.271, ...), kind=kLoop, calls=%fused_computation.14 | loop fusion | flops 14414336 | bytes 10512384 | tf_op jit(solution)/shard_map/reduce_sum | solution.py:247
  548.0 2.0 fusion.23
  550.1 2.0 collective-permute-start.5
  559.7 2.4 collective-permute-done.10
  562.8 3.0 collective-permute-done.11
  566.4 3.2 multiply_convert_fusion.5
  (323 shorter events, 96.9 us)
Async XLA Ops:
  7.2 248.0 %copy-start = (bf16[1024,1024]{1,0:T(8,128)(2,1)S(1)}, bf16[1024,1024]{1,0:T(8,128)(2,1)}, u32[]{:S(2)}) copy-start(bf16[1024,1024]{1,0:T(8,128)(2,1)} %param.28) | copy-start | bytes 6291460
  7.2 128.8 %all-gather.2.cloned.1.call-start = ((), (), s32[]{:S(2)}) async-start(), calls=%async_computation.3 | async-start | bytes 3276800 | tf_op jit(solution)/shard_map/all_gather | solution.py:130
  7.3 24.4 %collective-permute-start = (bf16[4,320,256]{2,1,0:T(8,128)(2,1)}, bf16[4,320,256]{2,1,0:T(8,128)(2,1)S(1)}, u32[]{:S(2)}, u32[]{:S(2)}) collective-permute-start(bf16[4,320,256]{2,1,0:T(8,128)(2,1)} %param.15), channel_id=1, source_target_pairs={{0,1},{1,2},{2,3},{3,0},{4,5},{5,6},{6,7},{7,4},{8,9},{9,10},{10,1... | collective-permute-start | bytes 1966088 | tf_op jit(solution)/shard_map/ppermute | solution.py:20
  10.4 57.5 %collective-permute-start.1 = (bf16[4,320,256]{2,1,0:T(8,128)(2,1)}, bf16[4,320,256]{2,1,0:T(8,128)(2,1)}, u32[]{:S(2)}, u32[]{:S(2)}) collective-permute-start(bf16[4,320,256]{2,1,0:T(8,128)(2,1)} %param.15), channel_id=1, source_target_pairs={{0,3},{1,0},{2,1},{3,2},{4,7},{5,4},{6,5},{7,6},{8,11},{9,8},{10,9... | collective-permute-start | bytes 1966088 | tf_op jit(solution)/shard_map/ppermute | solution.py:25
  12.5 231.5 %all-reduce.3.cloned.1.call-start = ((), (), s32[]{:S(2)}) async-start(), calls=%async_computation.2 | async-start | bytes 5242880 | tf_op jit(solution)/shard_map/psum | solution.py:161
  31.7 55.4 %collective-permute-start.2 = (bf16[4,320,256]{2,1,0:T(8,128)(2,1)S(1)}, bf16[4,320,256]{2,1,0:T(8,128)(2,1)}, u32[]{:S(2)}, u32[]{:S(2)}) collective-permute-start(bf16[4,320,256]{2,1,0:T(8,128)(2,1)S(1)} %collective-permute-done), channel_id=1, source_target_pairs={{0,1},{1,2},{2,3},{3,0},{4,5},{5,6},{6,7},{7,4},{8,9},{9,10},{10,1... | collective-permute-start | bytes 1966088 | tf_op jit(solution)/shard_map/ppermute | solution.py:20
  49.4 70.8 %copy-start.36 = (pred[4,320]{1,0:T(4,128)(4,1)}, pred[4,320]{1,0:T(4,128)(4,1)S(1)}, u32[]{:S(2)}) copy-start(pred[4,320]{1,0:T(4,128)(4,1)S(1)} %get-tuple-element.49) | copy-start | bytes 3844
  129.8 274.4 %all-reduce.5.cloned.1.call-start = ((), (), s32[]{:S(2)}) async-start(), calls=%async_computation.4 | async-start | bytes 5242880 | tf_op jit(solution)/shard_map/psum | solution.py:179
  299.5 9.0 %collective-permute-start.45 = (bf16[512,1024]{1,0:T(8,128)(2,1)S(1)}, bf16[512,1024]{1,0:T(8,128)(2,1)}, u32[]{:S(2)}, u32[]{:S(2)}) collective-permute-start(bf16[512,1024]{1,0:T(8,128)(2,1)S(1)} %dynamic-slice_convert_fusion), channel_id=1, source_target_pairs={{0,4},{4,0},{8,12},{12,8},{16,20},{20,16},{24,28},{28,24},{1,5},{5... | collective-permute-start | bytes 3145736 | tf_op jit(solution)/shard_map/ppermute | solution.py:61
  300.2 3.1 collective-permute-start.51
  300.7 4.1 collective-permute-start.42
  300.8 200.8 %reduce-scatter.3.cloned.1.call-start = ((), (), s32[]{:S(2)}) async-start(), calls=%async_computation.5 | async-start | bytes 3276800 | tf_op jit(solution)/shard_map/reduce_scatter | solution.py:181
  302.8 9.6 %collective-permute-start.36 = (bf16[512,1024]{1,0:T(8,128)(2,1)S(1)}, bf16[512,1024]{1,0:T(8,128)(2,1)S(1)}, u32[]{:S(2)}, u32[]{:S(2)}) collective-permute-start(bf16[512,1024]{1,0:T(8,128)(2,1)S(1)} %dynamic-slice_convert_fusion.1), channel_id=1, source_target_pairs={{0,4},{4,0},{8,12},{12,8},{16,20},{20,16},{24,28},{28,24},{1,5},{5... | collective-permute-start | bytes 3145736 | tf_op jit(solution)/shard_map/ppermute | solution.py:61
  303.3 3.6 collective-permute-start.52
  304.9 8.8 %collective-permute-start.43 = (bf16[1024]{0:T(1024)(128)(2,1)S(1)}, bf16[1024]{0:T(1024)(128)(2,1)S(1)}, u32[]{:S(2)}, u32[]{:S(2)}) collective-permute-start(bf16[1024]{0:T(1024)(128)(2,1)S(1)} %add_convert_fusion.22), channel_id=1, source_target_pairs={{0,8},{4,12},{8,0},{12,4},{16,24},{20,28},{24,16},{28,20},{1,9},{5... | collective-permute-start | bytes 6152 | tf_op jit(solution)/shard_map/ppermute | solution.py:61
  307.0 28.6 %collective-permute-start.53 = (bf16[1024]{0:T(1024)(128)(2,1)S(1)}, bf16[1024]{0:T(1024)(128)(2,1)S(1)}, u32[]{:S(2)}, u32[]{:S(2)}) collective-permute-start(bf16[1024]{0:T(1024)(128)(2,1)S(1)} %add_convert_fusion.18), channel_id=1, source_target_pairs={{0,16},{4,20},{8,24},{12,28},{16,0},{20,4},{24,8},{28,12},{1,17},{... | collective-permute-start | bytes 6152 | tf_op jit(solution)/shard_map/ppermute | solution.py:61
  310.9 14.9 %collective-permute-start.46 = (bf16[256,1024]{1,0:T(8,128)(2,1)S(1)}, bf16[256,1024]{1,0:T(8,128)(2,1)S(1)}, u32[]{:S(2)}, u32[]{:S(2)}) collective-permute-start(bf16[256,1024]{1,0:T(8,128)(2,1)S(1)} %dynamic-slice_convert_fusion.3), channel_id=1, source_target_pairs={{0,8},{4,12},{8,0},{12,4},{16,24},{20,28},{24,16},{28,20},{1,9},{5... | collective-permute-start | bytes 1572872 | tf_op jit(solution)/shard_map/ppermute | solution.py:61
  313.0 21.7 %collective-permute-start.37 = (bf16[256,1024]{1,0:T(8,128)(2,1)S(1)}, bf16[256,1024]{1,0:T(8,128)(2,1)S(1)}, u32[]{:S(2)}, u32[]{:S(2)}) collective-permute-start(bf16[256,1024]{1,0:T(8,128)(2,1)S(1)} %dynamic-slice_convert_fusion.4), channel_id=1, source_target_pairs={{0,8},{4,12},{8,0},{12,4},{16,24},{20,28},{24,16},{28,20},{1,9},{5... | collective-permute-start | bytes 1572872 | tf_op jit(solution)/shard_map/ppermute | solution.py:61
  313.6 31.2 %collective-permute-start.44 = (bf16[1024]{0:T(1024)(128)(2,1)S(1)}, bf16[1024]{0:T(1024)(128)(2,1)S(1)}, u32[]{:S(2)}, u32[]{:S(2)}) collective-permute-start(bf16[1024]{0:T(1024)(128)(2,1)S(1)} %add_convert_fusion.21), channel_id=1, source_target_pairs={{0,16},{4,20},{8,24},{12,28},{16,0},{20,4},{24,8},{28,12},{1,17},{... | collective-permute-start | bytes 6152 | tf_op jit(solution)/shard_map/ppermute | solution.py:61
  326.0 10.2 %collective-permute-start.47 = (bf16[128,1024]{1,0:T(8,128)(2,1)S(1)}, bf16[128,1024]{1,0:T(8,128)(2,1)S(1)}, u32[]{:S(2)}, u32[]{:S(2)}) collective-permute-start(bf16[128,1024]{1,0:T(8,128)(2,1)S(1)} %dynamic-slice_convert_fusion.6), channel_id=1, source_target_pairs={{0,16},{4,20},{8,24},{12,28},{16,0},{20,4},{24,8},{28,12},{1,17},{... | collective-permute-start | bytes 786440 | tf_op jit(solution)/shard_map/ppermute | solution.py:61
  334.9 9.2 %collective-permute-start.38 = (bf16[128,1024]{1,0:T(8,128)(2,1)S(1)}, bf16[128,1024]{1,0:T(8,128)(2,1)S(1)}, u32[]{:S(2)}, u32[]{:S(2)}) collective-permute-start(bf16[128,1024]{1,0:T(8,128)(2,1)S(1)} %dynamic-slice_convert_fusion.7), channel_id=1, source_target_pairs={{0,16},{4,20},{8,24},{12,28},{16,0},{20,4},{24,8},{28,12},{1,17},{... | collective-permute-start | bytes 786440 | tf_op jit(solution)/shard_map/ppermute | solution.py:61
  336.2 13.3 %collective-permute-start.48 = (bf16[128,1024]{1,0:T(8,128)(2,1)S(1)}, bf16[128,1024]{1,0:T(8,128)(2,1)S(1)}, u32[]{:S(2)}, u32[]{:S(2)}) collective-permute-start(bf16[128,1024]{1,0:T(8,128)(2,1)S(1)} %add_convert_fusion.4), channel_id=1, source_target_pairs={{0,16},{4,20},{8,24},{12,28},{16,0},{20,4},{24,8},{28,12},{1,17},{... | collective-permute-start | bytes 786440 | tf_op jit(solution)/shard_map/ppermute | solution.py:61
  344.2 62.5 %copy-start.28 = (f32[1280]{0:T(1024)S(1)}, f32[1280]{0:T(1024)}, u32[]{:S(2)}) copy-start(f32[1280]{0:T(1024)} %copy-done.26) | copy-start | bytes 15364
  344.2 62.5 %copy-start.33 = (f32[1280]{0:T(1024)S(1)}, f32[1280]{0:T(1024)}, u32[]{:S(2)}) copy-start(f32[1280]{0:T(1024)} %copy-done.31) | copy-start | bytes 15364
  344.2 62.5 %copy-start.43 = (f32[1024]{0:T(1024)S(1)}, f32[1024]{0:T(1024)}, u32[]{:S(2)}) copy-start(f32[1024]{0:T(1024)} %param.24) | copy-start | bytes 12292
  344.2 8.1 %collective-permute-start.39 = (bf16[128,1024]{1,0:T(8,128)(2,1)S(1)}, bf16[128,1024]{1,0:T(8,128)(2,1)S(1)}, u32[]{:S(2)}, u32[]{:S(2)}) collective-permute-start(bf16[128,1024]{1,0:T(8,128)(2,1)S(1)} %add_convert_fusion.5), channel_id=1, source_target_pairs={{0,16},{4,20},{8,24},{12,28},{16,0},{20,4},{24,8},{28,12},{1,17},{... | collective-permute-start | bytes 786440 | tf_op jit(solution)/shard_map/ppermute | solution.py:61
  350.4 112.2 %collective-permute-start.49 = (bf16[256,1024]{1,0:T(8,128)(2,1)}, bf16[256,1024]{1,0:T(8,128)(2,1)}, u32[]{:S(2)}, u32[]{:S(2)}) collective-permute-start(bf16[256,1024]{1,0:T(8,128)(2,1)} %maximum_select_fusion.9), channel_id=1, source_target_pairs={{0,8},{4,12},{8,0},{12,4},{16,24},{20,28},{24,16},{28,20},{1,9},{5... | collective-permute-start | bytes 1572872 | tf_op jit(solution)/shard_map/ppermute | solution.py:61
  353.2 112.1 %collective-permute-start.40 = (bf16[256,1024]{1,0:T(8,128)(2,1)}, bf16[256,1024]{1,0:T(8,128)(2,1)}, u32[]{:S(2)}, u32[]{:S(2)}) collective-permute-start(bf16[256,1024]{1,0:T(8,128)(2,1)} %maximum_select_fusion.8), channel_id=1, source_target_pairs={{0,8},{4,12},{8,0},{12,4},{16,24},{20,28},{24,16},{28,20},{1,9},{5... | collective-permute-start | bytes 1572872 | tf_op jit(solution)/shard_map/ppermute | solution.py:61
  437.2 129.2 %reduce-scatter.5.cloned.1.call-start = ((), (), s32[]{:S(2)}) async-start(), calls=%async_computation.6 | async-start | bytes 3276800 | tf_op jit(solution)/shard_map/reduce_scatter | solution.py:240
  437.2 31.8 %collective-permute-start.27 = (bf16[1024]{0:T(1024)(128)(2,1)S(1)}, bf16[1024]{0:T(1024)(128)(2,1)S(1)}, u32[]{:S(2)}, u32[]{:S(2)}) collective-permute-start(bf16[1024]{0:T(1024)(128)(2,1)S(1)} %copy-done.45), channel_id=1, source_target_pairs={{0,4},{4,0},{8,12},{12,8},{16,20},{20,16},{24,28},{28,24},{1,5},{5... | collective-permute-start | bytes 6152 | tf_op jit(solution)/shard_map/ppermute | solution.py:61
  437.3 31.8 %collective-permute-start.30 = (bf16[1024]{0:T(1024)(128)(2,1)S(1)}, bf16[1024]{0:T(1024)(128)(2,1)S(1)}, u32[]{:S(2)}, u32[]{:S(2)}) collective-permute-start(bf16[1024]{0:T(1024)(128)(2,1)S(1)} %copy-done.44), channel_id=1, source_target_pairs={{0,4},{4,0},{8,12},{12,8},{16,20},{20,16},{24,28},{28,24},{1,5},{5... | collective-permute-start | bytes 6152 | tf_op jit(solution)/shard_map/ppermute | solution.py:61
  437.8 34.9 %collective-permute-start.33 = (bf16[1024]{0:T(1024)(128)(2,1)S(1)}, bf16[1024]{0:T(1024)(128)(2,1)S(1)}, u32[]{:S(2)}, u32[]{:S(2)}) collective-permute-start(bf16[1024]{0:T(1024)(128)(2,1)S(1)} %get-tuple-element.27), channel_id=1, source_target_pairs={{0,4},{4,0},{8,12},{12,8},{16,20},{20,16},{24,28},{28,24},{1,5},{5... | collective-permute-start | bytes 6152 | tf_op jit(solution)/shard_map/ppermute | solution.py:61
  462.7 18.7 %collective-permute-start.21 = (bf16[128,1024]{1,0:T(8,128)(2,1)S(1)}, bf16[128,1024]{1,0:T(8,128)(2,1)S(1)}, u32[]{:S(2)}, u32[]{:S(2)}) collective-permute-start(bf16[128,1024]{1,0:T(8,128)(2,1)S(1)} %dynamic-slice_convert_fusion.8), channel_id=1, source_target_pairs={{0,4},{4,0},{8,12},{12,8},{16,20},{20,16},{24,28},{28,24},{1,5},{5... | collective-permute-start | bytes 786440 | tf_op jit(solution)/shard_map/ppermute | solution.py:61
  465.3 3.1 collective-permute-start.18
  468.5 21.5 %collective-permute-start.12 = (bf16[512,768]{0,1:T(8,128)(2,1)}, bf16[512,768]{0,1:T(8,128)(2,1)S(1)}, u32[]{:S(2)}, u32[]{:S(2)}) collective-permute-start(bf16[512,768]{0,1:T(8,128)(2,1)} %dynamic-slice_convert_fusion.2), channel_id=1, source_target_pairs={{0,4},{4,0},{8,12},{12,8},{16,20},{20,16},{24,28},{28,24},{1,5},{5... | collective-permute-start | bytes 2359304 | tf_op jit(solution)/shard_map/ppermute | solution.py:61
  469.0 57.0 %collective-permute-start.50 = (bf16[512,1024]{1,0:T(8,128)(2,1)S(1)}, bf16[512,1024]{1,0:T(8,128)(2,1)}, u32[]{:S(2)}, u32[]{:S(2)}) collective-permute-start(bf16[512,1024]{1,0:T(8,128)(2,1)S(1)} %maximum_select_fusion.4), channel_id=1, source_target_pairs={{0,4},{4,0},{8,12},{12,8},{16,20},{20,16},{24,28},{28,24},{1,5},{5... | collective-permute-start | bytes 3145736 | tf_op jit(solution)/shard_map/ppermute | solution.py:61
  469.1 3.6 collective-permute-start.19
  472.7 57.7 %collective-permute-start.41 = (bf16[512,1024]{1,0:T(8,128)(2,1)}, bf16[512,1024]{1,0:T(8,128)(2,1)}, u32[]{:S(2)}, u32[]{:S(2)}) collective-permute-start(bf16[512,1024]{1,0:T(8,128)(2,1)} %maximum_select_fusion.3), channel_id=1, source_target_pairs={{0,4},{4,0},{8,12},{12,8},{16,20},{20,16},{24,28},{28,24},{1,5},{5... | collective-permute-start | bytes 3145736 | tf_op jit(solution)/shard_map/ppermute | solution.py:61
  472.8 3.6 collective-permute-start.20
  476.4 3.6 collective-permute-start.28
  480.0 3.6 collective-permute-start.31
  481.4 9.7 %collective-permute-start.34 = (bf16[1024]{0:T(1024)(128)(2,1)S(1)}, bf16[1024]{0:T(1024)(128)(2,1)S(1)}, u32[]{:S(2)}, u32[]{:S(2)}) collective-permute-start(bf16[1024]{0:T(1024)(128)(2,1)S(1)} %add_convert_fusion.25), channel_id=1, source_target_pairs={{0,8},{4,12},{8,0},{12,4},{16,24},{20,28},{24,16},{28,20},{1,9},{5... | collective-permute-start | bytes 6152 | tf_op jit(solution)/shard_map/ppermute | solution.py:61
  483.6 5.0 collective-permute-start.22
  488.5 20.9 %collective-permute-start.29 = (bf16[1024]{0:T(1024)(128)(2,1)S(1)}, bf16[1024]{0:T(1024)(128)(2,1)S(1)}, u32[]{:S(2)}, u32[]{:S(2)}) collective-permute-start(bf16[1024]{0:T(1024)(128)(2,1)S(1)} %add_convert_fusion.30), channel_id=1, source_target_pairs={{0,16},{4,20},{8,24},{12,28},{16,0},{20,4},{24,8},{28,12},{1,17},{... | collective-permute-start | bytes 6152 | tf_op jit(solution)/shard_map/ppermute | solution.py:61
  490.0 4.3 collective-permute-start.23
  491.1 8.0 %collective-permute-start.13 = (bf16[256,768]{0,1:T(8,128)(2,1)S(1)}, bf16[256,768]{0,1:T(8,128)(2,1)S(1)}, u32[]{:S(2)}, u32[]{:S(2)}) collective-permute-start(bf16[256,768]{0,1:T(8,128)(2,1)S(1)} %dynamic-slice_convert_fusion.5), channel_id=1, source_target_pairs={{0,8},{4,12},{8,0},{12,4},{16,24},{20,28},{24,16},{28,20},{1,9},{5... | collective-permute-start | bytes 1179656 | tf_op jit(solution)/shard_map/ppermute | solution.py:61
  494.4 22.5 %collective-permute-start.32 = (bf16[1024]{0:T(1024)(128)(2,1)S(1)}, bf16[1024]{0:T(1024)(128)(2,1)S(1)}, u32[]{:S(2)}, u32[]{:S(2)}) collective-permute-start(bf16[1024]{0:T(1024)(128)(2,1)S(1)} %add_convert_fusion.27), channel_id=1, source_target_pairs={{0,16},{4,20},{8,24},{12,28},{16,0},{20,4},{24,8},{28,12},{1,17},{... | collective-permute-start | bytes 6152 | tf_op jit(solution)/shard_map/ppermute | solution.py:61
  500.2 7.6 %collective-permute-start.14 = (bf16[128,768]{0,1:T(8,128)(2,1)S(1)}, bf16[128,768]{0,1:T(8,128)(2,1)S(1)}, u32[]{:S(2)}, u32[]{:S(2)}) collective-permute-start(bf16[128,768]{0,1:T(8,128)(2,1)S(1)} %dynamic-slice_convert_fusion.9), channel_id=1, source_target_pairs={{0,16},{4,20},{8,24},{12,28},{16,0},{20,4},{24,8},{28,12},{1,17},{... | collective-permute-start | bytes 589832 | tf_op jit(solution)/shard_map/ppermute | solution.py:61
  507.8 4.3 collective-permute-start.24
  509.5 5.7 collective-permute-start.15
  512.1 8.2 %collective-permute-start.35 = (bf16[1024]{0:T(1024)(128)(2,1)S(1)}, bf16[1024]{0:T(1024)(128)(2,1)S(1)}, u32[]{:S(2)}, u32[]{:S(2)}) collective-permute-start(bf16[1024]{0:T(1024)(128)(2,1)S(1)} %add_convert_fusion.24), channel_id=1, source_target_pairs={{0,16},{4,20},{8,24},{12,28},{16,0},{20,4},{24,8},{28,12},{1,17},{... | collective-permute-start | bytes 6152 | tf_op jit(solution)/shard_map/ppermute | solution.py:61
  515.2 5.0 collective-permute-start.25
  516.8 7.8 %collective-permute-start.16 = (bf16[256,768]{0,1:T(8,128)(2,1)S(1)}, bf16[256,768]{0,1:T(8,128)(2,1)S(1)}, u32[]{:S(2)}, u32[]{:S(2)}) collective-permute-start(bf16[256,768]{0,1:T(8,128)(2,1)S(1)} %maximum_select_fusion.11), channel_id=1, source_target_pairs={{0,8},{4,12},{8,0},{12,4},{16,24},{20,28},{24,16},{28,20},{1,9},{5... | collective-permute-start | bytes 1179656 | tf_op jit(solution)/shard_map/ppermute | solution.py:61
  520.2 4.7 collective-permute-start.26
  524.8 11.8 %collective-permute-start.17 = (bf16[512,768]{0,1:T(8,128)(2,1)S(1)}, bf16[512,768]{0,1:T(8,128)(2,1)}, u32[]{:S(2)}, u32[]{:S(2)}) collective-permute-start(bf16[512,768]{0,1:T(8,128)(2,1)S(1)} %maximum_select_fusion.6), channel_id=1, source_target_pairs={{0,4},{4,0},{8,12},{12,8},{16,20},{20,16},{24,28},{28,24},{1,5},{5... | collective-permute-start | bytes 2359304 | tf_op jit(solution)/shard_map/ppermute | solution.py:61
  548.0 4.2 collective-permute-start.7
  550.1 3.7 collective-permute-start.5
  552.1 4.7 collective-permute-start.3
  552.1 4.6 collective-permute-start.8
  553.8 5.9 %collective-permute-start.6 = (bf16[1280]{0:T(1024)(128)(2,1)S(1)}, bf16[1280]{0:T(1024)(128)(2,1)S(1)}, u32[]{:S(2)}, u32[]{:S(2)}) collective-permute-start(bf16[1280]{0:T(1024)(128)(2,1)S(1)} %add_convert_fusion.14), channel_id=1, source_target_pairs={{0,2},{1,3},{2,0},{3,1},{4,6},{5,7},{6,4},{7,5},{8,10},{9,11},{10,... | collective-permute-start | bytes 7688 | tf_op jit(solution)/shard_map/ppermute | solution.py:61
  556.7 1.7 collective-permute-start.9
  556.8 5.9 %collective-permute-start.4 = (bf16[1280]{0:T(1024)(128)(2,1)S(1)}, bf16[1280]{0:T(1024)(128)(2,1)S(1)}, u32[]{:S(2)}, u32[]{:S(2)}) collective-permute-start(bf16[1280]{0:T(1024)(128)(2,1)S(1)} %add_convert_fusion.16), channel_id=1, source_target_pairs={{0,2},{1,3},{2,0},{3,1},{4,6},{5,7},{6,4},{7,5},{8,10},{9,11},{10,... | collective-permute-start | bytes 7688 | tf_op jit(solution)/shard_map/ppermute | solution.py:61
  558.5 3.7 collective-permute-start.10
  562.1 3.7 collective-permute-start.11
  (54 other events, 514.1 us)
Sparse Core Ops, SparseCore 0:
  12.6 85.1 all-gather.1
  129.9 113.9 all-reduce.2
  301.0 103.1 all-reduce.4
  437.3 51.2 reduce-scatter.2
  504.4 49.9 reduce-scatter.4
